TPU v7x, 32 devices: a whole 2x2x4 slice. The times are simulated.
32 devices in a mesh: grp: 4 (over y, x), blk: 8 (over z, core).
Axes of the slice: x: 2, y: 2, z: 4, core: 2. Of those that a mesh axis runs over, the one named last changes fastest.
Arguments:
- data: bfloat16 [256, 65536], P('blk'), may hold values from -8 to 8
- labels: int32 [256], P('blk'), may hold values from -1 to 1, as said below
- order: int32 [8, 4], P('blk'), may hold values from 0 to 3, each once within a row
- reg_index: int32 [4], P('grp'), parts along dimension 0, may hold values from 0 to 5
Outputs:
- dual: float32 [1024], P(('grp', 'blk')), parts along dimension 0
- margins: float32 [1024], P(('grp', 'blk')), parts along dimension 0
- gap: float32 [4], P('grp'), parts along dimension 0
There are 4 independent parts, one for each index of `grp`. A program takes and returns all parts, laid end to end along the dimension named above; an argument that names none is the same for every part. Nothing has to cross between parts.
Inputs may be any that keep to these rules, and one draw needn't show every extreme that they name: `labels`: each entry is -1 or 1.
All inputs are finite; a program needn't handle non-finite values.
Results may differ from a plain program's by a relative error of at most 0.00055.
Values sent between devices are 32-bit elements; how exact they have to be, the bound alone decides.
No kernel may reach another device: no remote copies, remote signals or barrier semaphores. Data moves between devices by JAX's collectives and lax.ppermute only.
A program may use at most 64 MiB of HBM per device.

v0:
```python
import math
import jax
import jax.numpy as jnp
from jax import lax
from jax.sharding import PartitionSpec as P

NBLOCKS = 4
ROUNDS = 2


def local_round(shard_data, signs, dual, order_row, weights, reg_total, sigma_prime, squared):
    block_rows = shard_data.shape[0] // NBLOCKS
    feature_scale = 1.0 / math.sqrt(shard_data.shape[1])
    local_weights = weights
    dual_change = jnp.zeros_like(dual)
    for position in range(NBLOCKS):
        offset = order_row[position] * block_rows
        block_data = lax.dynamic_slice_in_dim(shard_data, offset, block_rows, 0)
        block_signs = lax.dynamic_slice_in_dim(signs, offset, block_rows, 0)
        block_dual = lax.dynamic_slice_in_dim(dual, offset, block_rows, 0)
        block_change = lax.dynamic_slice_in_dim(dual_change, offset, block_rows, 0)
        block_norms = lax.dynamic_slice_in_dim(squared, offset, block_rows, 0)
        rounded = local_weights.astype(jnp.bfloat16)
        score = feature_scale * jnp.dot(block_data, rounded, preferred_element_type=jnp.float32)
        current = block_dual + block_change
        updated = jnp.clip(
            current + reg_total * (1.0 - block_signs * score) / (sigma_prime * block_norms),
            0.0,
            1.0,
        )
        change = updated - current
        dual_change = lax.dynamic_update_slice_in_dim(dual_change, block_change + change, offset, 0)
        coefficient = (block_signs * change).astype(jnp.bfloat16)
        local_weights = local_weights + sigma_prime * feature_scale / reg_total * jnp.dot(
            coefficient, block_data, preferred_element_type=jnp.float32
        )
    return dual_change


def shards(data, labels, order, reg_index):
    group_size = lax.axis_size("blk")
    row_count = data.shape[0]
    feature_count = data.shape[1]
    samples_all = row_count * group_size
    feature_scale = 1.0 / math.sqrt(feature_count)
    reg_strength = 0.04 * jnp.exp(0.5 * math.log(2.0) * reg_index[0].astype(jnp.float32))
    reg_total = reg_strength * samples_all
    sigma_prime = jnp.float32(group_size)
    signs = labels.astype(jnp.float32)
    squared = (
        jnp.einsum("rf,rf->r", data, data, preferred_element_type=jnp.float32) / feature_count
        + 1e-06
    )
    weights = jnp.zeros((feature_count,), jnp.float32)
    dual = jnp.zeros((row_count,), jnp.float32)
    for round_index in range(ROUNDS):
        dual_change = local_round(
            data, signs, dual, order[0], weights, reg_total, sigma_prime, squared
        )
        coefficient = (signs * dual_change).astype(jnp.bfloat16)
        delta = (
            feature_scale
            / reg_total
            * jnp.dot(coefficient, data, preferred_element_type=jnp.float32)
        )
        weights = weights + lax.psum(delta, "blk")
        dual = dual + dual_change
    margins = feature_scale * jnp.dot(
        data, weights.astype(jnp.bfloat16), preferred_element_type=jnp.float32
    )
    hinge = jnp.maximum(0.0, 1.0 - signs * margins)
    hinge_total, dual_total = lax.psum((jnp.sum(hinge), jnp.sum(dual)), "blk")
    gap = reg_strength * jnp.sum(weights * weights) + (hinge_total - dual_total) / samples_all
    return (dual, margins, gap.reshape(1))


def solution(mesh):
    placed = (P("blk", None), P("blk"), P("blk", None), P("grp"))
    return jax.shard_map(
        shards,
        mesh=mesh,
        in_specs=placed,
        out_specs=(P(("grp", "blk")), P(("grp", "blk")), P("grp")),
        check_vma=False,
    )
```

profile of v0, /device:TPU:0, one launch (start us, length us, event | category | flops | bytes accessed | tf_op | source)
XLA Modules:
  0.0 192.1 jit_solution(11065774794570149796)
XLA Ops:
  7.2 0.0 all-reduce.4.cloned.1.call-start
  7.2 1.4 fusion.134
  11.8 0.7 convert_element_type.59
  12.5 3.1 %fusion = f32[32]{0:T(128)S(1)} fusion(bf16[32,65536]{1,0:T(8,128)(2,1)} %param.4), kind=kLoop, calls=%fused_computation.1 | loop fusion | flops 6291424 | bytes 4194432 | tf_op jit(solution)/shard_map/rf,rf->r/dot_general | solution.py:51
  15.7 0.1 fusion.135
  15.7 2.1 %fusion.6 = f32[8]{0:T(128)S(1)} fusion(f32[8]{0:T(128)S(1)} %get-tuple-element.15, bf16[32,65536]{1,0:T(8,128)(2,1)} %param.4, s32[]{:T(128)S(6)} %select_n.8, f32[32]{0:T(128)S(1)} %multiply_add_fusion.3, f32[]{:T(128)} %bitcast), kind=kOutput, calls=%fused_computation.15 | convolution fusion | flops 1048632 | bytes 1050208 | tf_op jit(solution)/shard_map/dot_general | solution.py:24
  17.8 1.7 fusion.83
  19.5 0.2 dynamic_update_slice.24
  19.7 0.0 copy-start
  19.7 0.1 reshape.40
  19.9 2.2 %fusion.14 = f32[8]{0:T(128)S(1)} fusion(f32[8]{0:T(128)S(1)} %get-tuple-element.14, bf16[65536,1]{0,1:T(2,128)(2,1)S(1)} %reshape.40, bf16[32,65536]{1,0:T(8,128)(2,1)} %param.4, s32[]{:T(128)S(6)} %select_n.9, f32[32]{0:T(128)S(1)} %multiply_add_fusion.3, f32[]{:T(128)} %bitcast, f32[32]{0:T(128)S(1)} %dynamic_update_slice.24), kind=kOutput, calls=%fused_computation.23 | convolution fusion | flops 1048648 | bytes 1181312 | tf_op jit(solution)/shard_map/dot_general | solution.py:24
  22.1 0.0 copy-start.3
  22.1 0.2 add_dynamic-update-slice_fusion.3
  22.3 1.6 fusion.77
  24.0 0.1 reshape.44
  24.1 0.0 copy-done
  24.1 0.9 fusion.22
  25.0 0.2 add_dynamic-update-slice_fusion.2
  25.1 0.4 fusion.71
  25.6 0.1 add_convert_fusion.1
  25.7 0.1 reshape.48
  25.8 2.1 %fusion.31 = f32[8]{0:T(128)S(1)} fusion(bf16[65536,1]{0,1:T(2,128)(2,1)S(1)} %reshape.48, bf16[32,65536]{1,0:T(8,128)(2,1)} %param.4, s32[]{:T(128)S(6)} %select_n.11, f32[32]{0:T(128)S(1)} %add_dynamic-update-slice_fusion.2, f32[32]{0:T(128)S(1)} %multiply_add_fusion.3, f32[]{:T(128)} %bitcast, f32[32]{0:T(128)S(1)} %convert_element_type.59), kind=kOutput, calls=%fused_computation.40 | convolution fusion | flops 1048656 | bytes 1181312 | tf_op jit(solution)/shard_map/dot_general | solution.py:24
  27.9 0.2 dynamic_update_slice.27
  28.1 0.0 copy-done.3
  28.1 2.8 %fusion.108 = f32[1,65536]{1,0:T(1,128)S(1)} fusion(bf16[32,65536]{1,0:T(8,128)(2,1)} %param.4, f32[32]{0:T(128)S(1)} %dynamic_update_slice.27, s32[32]{0:T(128)S(1)} %copy-done.3), kind=kOutput, calls=%fused_computation.128 | convolution fusion | flops 4194400 | bytes 4456704 | tf_op jit(solution)/shard_map/dot_general | solution.py:64
  31.0 0.7 broadcast_multiply_fusion.1
  31.7 0.0 all-reduce.4.cloned.1.call-update
  31.7 0.0 all-reduce.6.cloned.1.call-start
  31.8 58.2 %all-reduce.4.cloned.1.call-done = f32[65536]{0:T(1024)} async-done(((f32[65536]{0:T(1024)}), f32[65536]{0:T(1024)}) %all-reduce.4.cloned.1.call-update) | async-done | bytes 262160 | tf_op jit(solution)/shard_map/psum | solution.py:66
  90.0 0.0 copy-start.2
  90.0 1.0 convert_element_type.68
  91.1 0.1 reshape.52
  91.2 2.1 %fusion.39 = f32[8]{0:T(128)S(1)} fusion(f32[8]{0:T(128)S(1)} %get-tuple-element.15, bf16[65536,1]{0,1:T(2,128)(2,1)S(1)} %reshape.52, bf16[32,65536]{1,0:T(8,128)(2,1)} %param.4, s32[]{:T(128)S(6)} %select_n.8, f32[32]{0:T(128)S(1)} %dynamic_update_slice.27, f32[32]{0:T(128)S(1)} %multiply_add_fusion.3, f32[]{:T(128)} %bitcast), kind=kOutput, calls=%fused_computation.48 | convolution fusion | flops 1048648 | bytes 1181312 | tf_op jit(solution)/shard_map/dot_general | solution.py:24
  93.3 1.7 fusion.80
  95.0 0.2 dynamic_update_slice.28
  95.2 0.0 copy-start.1
  95.2 1.1 fusion.87
  96.3 0.1 reshape.56
  96.5 2.1 %fusion.47 = f32[8]{0:T(128)S(1)} fusion(f32[8]{0:T(128)S(1)} %get-tuple-element.14, bf16[65536,1]{0,1:T(2,128)(2,1)S(1)} %reshape.56, bf16[32,65536]{1,0:T(8,128)(2,1)} %param.4, s32[]{:T(128)S(6)} %select_n.9, f32[32]{0:T(128)S(1)} %dynamic_update_slice.27, f32[32]{0:T(128)S(1)} %multiply_add_fusion.3, f32[]{:T(128)} %bitcast, f32[32]{0:T(128)S(1)} %dynamic_update_slice.28), kind=kOutput, calls=%fused_computation.56 | convolution fusion | flops 1048656 | bytes 1181344 | tf_op jit(solution)/shard_map/dot_general | solution.py:24
  98.6 0.2 add_dynamic-update-slice_fusion.1
  98.8 1.7 fusion.74
  100.4 0.0 copy-done.2
  100.5 0.1 reshape.60
  100.6 0.0 copy-done.1
  100.6 0.9 fusion.55
  101.5 0.2 add_dynamic-update-slice_fusion
  101.7 0.4 fusion.68
  102.1 0.1 add_convert_fusion
  102.2 0.1 reshape.64
  102.4 0.9 fusion.64
  103.2 0.2 dynamic_update_slice.31
  103.4 2.8 %fusion.103 = f32[1,65536]{1,0:T(1,128)S(1)} fusion(bf16[32,65536]{1,0:T(8,128)(2,1)} %param.4, f32[32]{0:T(128)S(1)} %dynamic_update_slice.31, s32[32]{0:T(128)S(1)} %copy-done.3), kind=kOutput, calls=%fused_computation.123 | convolution fusion | flops 4194400 | bytes 4456704 | tf_op jit(solution)/shard_map/dot_general | solution.py:64
  106.3 0.7 broadcast_multiply_fusion
  107.0 0.0 all-reduce.6.cloned.1.call-update
  107.0 1.1 fusion.133
  108.1 53.5 %all-reduce.6.cloned.1.call-done = f32[65536]{0:T(1024)} async-done(((f32[65536]{0:T(1024)}), f32[65536]{0:T(1024)}) %all-reduce.6.cloned.1.call-update) | async-done | bytes 262160 | tf_op jit(solution)/shard_map/psum | solution.py:66
  161.6 1.7 multiply_reduce_fusion
  163.3 0.1 reshape.68
  163.5 4.5 %maximum_reduce_fusion = (f32[]{:T(128)}, f32[32]{0:T(128)}) fusion(s32[32]{0:T(128)S(1)} %copy-done.3, bf16[65536,1]{0,1:T(2,128)(2,1)S(1)} %reshape.68, bf16[32,65536]{1,0:T(8,128)(2,1)} %param.4), kind=kOutput, calls=%fused_computation.133 | convolution fusion | flops 4194495 | bytes 4325636 | tf_op jit(solution)/shard_map/dot_general | solution.py:68
  168.0 14.3 %all-reduce = (f32[]{:T(128)}, f32[]{:T(128)}) all-reduce(f32[]{:T(128)} %get-tuple-element.16, f32[]{:T(128)} %get-tuple-element.5), channel_id=1, replica_groups=mesh['grp'=4,'blk'=8] {'blk'}, use_global_device_ids=true, to_apply=%region_4.5 | all-reduce | flops 2 | bytes 16 | tf_op jit(solution)/shard_map/psum | solution.py:72
  (6 shorter events, 0.1 us)
Async XLA Ops:
  7.2 82.9 %all-reduce.4.cloned.1.call-start = ((), (), s32[]{:S(2)}) async-start(), calls=%async_computation | async-start | bytes 524288 | tf_op jit(solution)/shard_map/psum | solution.py:66
  19.7 4.4 %copy-start = (bf16[32,65536]{1,0:T(8,128)(2,1)S(1)}, bf16[32,65536]{1,0:T(8,128)(2,1)}, u32[]{:S(2)}) copy-start(bf16[32,65536]{1,0:T(8,128)(2,1)} %param.4) | copy-start | bytes 12582916
  22.1 6.0 %copy-start.3 = (s32[32]{0:T(128)S(1)}, s32[32]{0:T(128)}, u32[]{:S(2)}) copy-start(s32[32]{0:T(128)} %param.5) | copy-start | bytes 388
  31.7 129.9 %all-reduce.6.cloned.1.call-start = ((), (), s32[]{:S(2)}) async-start(), calls=%async_computation.1 | async-start | bytes 524288 | tf_op jit(solution)/shard_map/psum | solution.py:66
  90.0 10.4 %copy-start.2 = (f32[65536]{0:T(1024)S(1)}, f32[65536]{0:T(1024)}, u32[]{:S(2)}) copy-start(f32[65536]{0:T(1024)} %all-reduce.4.cloned.1.call-done) | copy-start | bytes 786436
  95.2 5.4 %copy-start.1 = (bf16[32,65536]{1,0:T(8,128)(2,1)S(1)}, bf16[32,65536]{1,0:T(8,128)(2,1)}, u32[]{:S(2)}) copy-start(bf16[32,65536]{1,0:T(8,128)(2,1)} %param.4) | copy-start | bytes 12582916
Sparse Core Ops, SparseCore 0:
  31.8 58.1 all-reduce.3
  107.1 54.4 all-reduce.5
where the time goes:
time: 193 us; the launch traced here: 192 us
  waiting for transfers between devices  112 us (58%)
  matrix products  30.8 us (16%)
  between operations  20.5 us (11%)
  blocking collectives  14.3 us (7%)
  other arithmetic  11.1 us (6%)
  local copies, waits for them, and re-layouts  3.5 us (2%)
    psum x2, waiting for transfers between devices, shards(): weights = weights + lax.psum(delta, 'blk')  112 us
    psum x1, blocking collectives, shards(): hinge_total, dual_total = lax.psum((jnp.sum(hinge), jnp.sum(dual)), 'blk')  14.3 us
    dot_general x8, matrix products, local_round(): jnp.dot(block_data, rounded, preferred_element_type=jnp.float32)  13.1 us
    dot_general x6, matrix products, local_round(): jnp.dot(coefficient, block_data, preferred_element_type=jnp.float32)  7.46 us
    dot_general x2, matrix products, shards(): jnp.dot(coefficient, data, preferred_element_type=jnp.float32)  5.69 us
    dot_general x1, matrix products, shards(): jnp.dot(data, weights.astype(jnp.bfloat16), preferred_element_type=jnp.fl...  4.52 us
  transfers between devices with their start and end apart: 2, of which 2 were waited for; matrix products, arithmetic and copies ran while one was open for 1% of the time, Pallas kernels for 0%

commit v1 on v0

--- a/solution.py
+++ b/solution.py
@@ -6,6 +6,12 @@
 
 NBLOCKS = 4
 ROUNDS = 2
+
+
+def gather_and_add(x, axis):
+    parts = lax.all_gather(x, axis, axis=0, tiled=False)
+    result = parts.sum(axis=0)
+    return result
 
 
 def local_round(shard_data, signs, dual, order_row, weights, reg_total, sigma_prime, squared):
@@ -63,7 +69,7 @@
             / reg_total
             * jnp.dot(coefficient, data, preferred_element_type=jnp.float32)
         )
-        weights = weights + lax.psum(delta, "blk")
+        weights = weights + gather_and_add(delta, "blk")
         dual = dual + dual_change
     margins = feature_scale * jnp.dot(
         data, weights.astype(jnp.bfloat16), preferred_element_type=jnp.float32

time: 193 us -> 148 us (0.77)
  waiting for transfers between devices: 112 us -> 59.6 us
  local copies, waits for them, and re-layouts: 3.5 us -> 7.5 us
  matrix products: 30.8 us -> 34.4 us
  other arithmetic: 11.1 us -> 9.1 us
    psum x2 -> x0, waiting for transfers between devices: 112 us -> none  [shards(): weights = weights + lax.psum(delta, 'blk')]
    all_gather x0 -> x2, waiting for transfers between devices: none -> 59.6 us  [gather_and_add(): parts = lax.all_gather(x, axis, axis=0, tiled=False)]
    all_gather x0 -> x2, local copies, waits for them, and re-layouts: none -> 3.93 us  [gather_and_add(): parts = lax.all_gather(x, axis, axis=0, tiled=False)]
    dot_general x8, matrix products: 13.1 us -> 15.5 us  [local_round(): jnp.dot(block_data, rounded, preferred_element_type=jnp.float32)]
    convert_element_type x7, other arithmetic: 2.38 us -> 0.25 us  [local_round(): rounded = local_weights.astype(jnp.bfloat16)]
where the time goes in v1:
time: 148 us; the launch traced here: 147 us
  waiting for transfers between devices  59.6 us (40%)
  matrix products  34.4 us (23%)
  between operations  20.8 us (14%)
  blocking collectives  15.9 us (11%)
  other arithmetic  9.1 us (6%)
  local copies, waits for them, and re-layouts  7.5 us (5%)
    all_gather x2, waiting for transfers between devices, gather_and_add(): parts = lax.all_gather(x, axis, axis=0, tiled=False)  59.6 us
    psum x1, blocking collectives, shards(): hinge_total, dual_total = lax.psum((jnp.sum(hinge), jnp.sum(dual)), 'blk')  15.9 us
    dot_general x8, matrix products, local_round(): jnp.dot(block_data, rounded, preferred_element_type=jnp.float32)  15.5 us
    dot_general x6, matrix products, local_round(): jnp.dot(coefficient, block_data, preferred_element_type=jnp.float32)  8.71 us
    dot_general x2, matrix products, shards(): jnp.dot(coefficient, data, preferred_element_type=jnp.float32)  5.69 us
    dot_general x1, matrix products, shards(): jnp.dot(data, weights.astype(jnp.bfloat16), preferred_element_type=jnp.fl...  4.49 us
    all_gather x2, local copies, waits for them, and re-layouts, gather_and_add(): parts = lax.all_gather(x, axis, axis=0, tiled=False)  3.93 us
    dot_general x1, other arithmetic, shards(): jnp.einsum('rf,rf->r', data, data, preferred_element_type=jnp.float32)  3.1 us
  transfers between devices with their start and end apart: 2, of which 2 were waited for; matrix products, arithmetic and copies ran while one was open for 1% of the time, Pallas kernels for 0%

profile of v1, /device:TPU:0, one launch (start us, length us, event | category | flops | bytes accessed | tf_op | source)
XLA Modules:
  0.0 147.4 jit_solution(1704334198066819783)
XLA Ops:
  7.2 0.0 all-gather.5.cloned.1.call-start
  7.2 1.5 %fusion.134 = (s32[1,1]{1,0:T(1,128)}, s32[1,1]{1,0:T(1,128)}, s32[1,1]{1,0:T(1,128)}, s32[1,1]{1,0:T(1,128)}) fusion(s32[1,4]{1,0:T(1,128)} %param.6), kind=kLoop, calls=%fused_computation.164 | loop fusion | bytes 32 | tf_op jit(solution)/shard_map/slice | solution.py:23
  10.7 0.7 convert_element_type.59
  12.0 3.1 %fusion = f32[32]{0:T(128)S(1)} fusion(bf16[32,65536]{1,0:T(8,128)(2,1)} %param.4), kind=kLoop, calls=%fused_computation.1 | loop fusion | flops 6291424 | bytes 4194432 | tf_op jit(solution)/shard_map/rf,rf->r/dot_general | solution.py:57
  15.2 0.1 fusion.135
  15.3 2.1 %fusion.6 = f32[8]{0:T(128)S(1)} fusion(f32[8]{0:T(128)S(1)} %get-tuple-element.15, bf16[32,65536]{1,0:T(8,128)(2,1)} %param.4, s32[]{:T(128)S(6)} %select_n.8, f32[32]{0:T(128)S(1)} %multiply_add_fusion.3, f32[]{:T(128)} %bitcast), kind=kOutput, calls=%fused_computation.15 | convolution fusion | flops 1048632 | bytes 1050208 | tf_op jit(solution)/shard_map/dot_general | solution.py:30
  17.3 1.7 %fusion.83 = f32[1,65536]{1,0:T(1,128)S(1)} fusion(bf16[32,65536]{1,0:T(8,128)(2,1)} %param.4, s32[]{:T(128)S(6)} %select_n.8, f32[8]{0:T(128)S(1)} %get-tuple-element.15, f32[8]{0:T(128)S(1)} %fusion.6), kind=kOutput, calls=%fused_computation.93 | convolution fusion | flops 1048592 | bytes 1310788 | tf_op jit(solution)/shard_map/dot_general | solution.py:40
  19.0 0.1 reshape.42
  19.2 0.2 dynamic_update_slice.24
  19.4 2.1 %fusion.14 = f32[8]{0:T(128)S(1)} fusion(f32[8]{0:T(128)S(1)} %get-tuple-element.14, bf16[65536,1]{0,1:T(2,128)(2,1)S(1)} %reshape.42, bf16[32,65536]{1,0:T(8,128)(2,1)} %param.4, s32[]{:T(128)S(6)} %select_n.9, f32[32]{0:T(128)S(1)} %multiply_add_fusion.3, f32[]{:T(128)} %bitcast, f32[32]{0:T(128)S(1)} %dynamic_update_slice.24), kind=kOutput, calls=%fused_computation.23 | convolution fusion | flops 1048648 | bytes 1181312 | tf_op jit(solution)/shard_map/dot_general | solution.py:30
  21.5 0.0 copy-start.1
  21.5 1.7 %fusion.77 = f32[1,65536]{1,0:T(1,128)S(1)} fusion(bf16[32,65536]{1,0:T(8,128)(2,1)} %param.4, s32[]{:T(128)S(6)} %select_n.9, f32[8]{0:T(128)S(1)} %get-tuple-element.14, f32[8]{0:T(128)S(1)} %fusion.14), kind=kOutput, calls=%fused_computation.87 | convolution fusion | flops 1048592 | bytes 1310788 | tf_op jit(solution)/shard_map/dot_general | solution.py:40
  23.2 0.2 add_dynamic-update-slice_fusion.3
  23.4 0.1 reshape.46
  23.5 2.1 %fusion.22 = f32[8]{0:T(128)S(1)} fusion(f32[8]{0:T(128)S(1)} %get-tuple-element.13, bf16[65536,1]{0,1:T(2,128)(2,1)S(1)} %reshape.46, bf16[32,65536]{1,0:T(8,128)(2,1)} %param.4, s32[]{:T(128)S(6)} %select_n.10, f32[32]{0:T(128)S(1)} %multiply_add_fusion.3, f32[]{:T(128)} %bitcast, f32[32]{0:T(128)S(1)} %add_dynamic-update-slice_fusion.3), kind=kOutput, calls=%fused_computation.31 | convolution fusion | flops 1048648 | bytes 1181312 | tf_op jit(solution)/shard_map/dot_general | solution.py:30
  25.6 1.7 %fusion.71 = f32[1,65536]{1,0:T(1,128)S(1)} fusion(bf16[32,65536]{1,0:T(8,128)(2,1)} %param.4, s32[]{:T(128)S(6)} %select_n.10, f32[8]{0:T(128)S(1)} %get-tuple-element.13, f32[8]{0:T(128)S(1)} %fusion.22), kind=kOutput, calls=%fused_computation.81 | convolution fusion | flops 1048592 | bytes 1310788 | tf_op jit(solution)/shard_map/dot_general | solution.py:40
  27.3 0.2 add_dynamic-update-slice_fusion.2
  28.1 0.1 add_convert_fusion.1
  28.2 0.1 reshape.50
  28.3 2.1 %fusion.31 = f32[8]{0:T(128)S(1)} fusion(bf16[65536,1]{0,1:T(2,128)(2,1)S(1)} %reshape.50, bf16[32,65536]{1,0:T(8,128)(2,1)} %param.4, s32[]{:T(128)S(6)} %select_n.11, f32[32]{0:T(128)S(1)} %add_dynamic-update-slice_fusion.2, f32[32]{0:T(128)S(1)} %multiply_add_fusion.3, f32[]{:T(128)} %bitcast, f32[32]{0:T(128)S(1)} %convert_element_type.59), kind=kOutput, calls=%fused_computation.40 | convolution fusion | flops 1048656 | bytes 1181312 | tf_op jit(solution)/shard_map/dot_general | solution.py:30
  30.4 0.2 dynamic_update_slice.27
  30.6 0.0 copy-done.1
  30.6 2.8 %fusion.108 = f32[1,65536]{1,0:T(1,128)S(1)} fusion(bf16[32,65536]{1,0:T(8,128)(2,1)} %param.4, f32[32]{0:T(128)S(1)} %dynamic_update_slice.27, s32[32]{0:T(128)S(1)} %copy-done.1), kind=kOutput, calls=%fused_computation.128 | convolution fusion | flops 4194400 | bytes 4456704 | tf_op jit(solution)/shard_map/dot_general | solution.py:70
  33.5 0.7 broadcast_multiply_fusion.1
  34.3 0.0 all-gather.5.cloned.1.call-update
  34.3 0.0 all-gather.7.cloned.1.call-start
  34.3 32.0 %all-gather.5.cloned.1.call-done = f32[524288]{0:T(1024)} async-done(((f32[65536]{0:T(1024)}), f32[524288]{0:T(1024)}) %all-gather.5.cloned.1.call-update) | async-done | bytes 2097168 | tf_op jit(solution)/shard_map/all_gather | solution.py:12
  66.3 2.0 %reshape.34 = f32[8,65536]{1,0:T(8,128)S(1)} reshape(f32[524288]{0:T(1024)} %all-gather.5.cloned.1.call-done) | data formatting | bytes 4194304 | tf_op jit(solution)/shard_map/all_gather | solution.py:12
  68.3 0.5 reduce_sum.45
  68.8 0.1 reshape.54
  68.9 2.1 %fusion.39 = f32[8]{0:T(128)S(1)} fusion(f32[8]{0:T(128)S(1)} %get-tuple-element.15, bf16[65536,1]{0,1:T(2,128)(2,1)S(1)} %reshape.54, bf16[32,65536]{1,0:T(8,128)(2,1)} %param.4, s32[]{:T(128)S(6)} %select_n.8, f32[32]{0:T(128)S(1)} %dynamic_update_slice.27, f32[32]{0:T(128)S(1)} %multiply_add_fusion.3, f32[]{:T(128)} %bitcast), kind=kOutput, calls=%fused_computation.48 | convolution fusion | flops 1048648 | bytes 1181312 | tf_op jit(solution)/shard_map/dot_general | solution.py:30
  71.0 1.7 %fusion.80 = f32[1,65536]{1,0:T(1,128)S(1)} fusion(bf16[32,65536]{1,0:T(8,128)(2,1)} %param.4, s32[]{:T(128)S(6)} %select_n.8, f32[8]{0:T(128)S(1)} %get-tuple-element.15, f32[8]{0:T(128)S(1)} %fusion.39), kind=kOutput, calls=%fused_computation.90 | convolution fusion | flops 1048592 | bytes 1310788 | tf_op jit(solution)/shard_map/dot_general | solution.py:40
  72.7 0.1 reshape.58
  72.9 0.2 dynamic_update_slice.28
  73.1 0.0 copy-start
  73.1 2.2 %fusion.47 = f32[8]{0:T(128)S(1)} fusion(f32[8]{0:T(128)S(1)} %get-tuple-element.14, bf16[65536,1]{0,1:T(2,128)(2,1)S(1)} %reshape.58, bf16[32,65536]{1,0:T(8,128)(2,1)} %param.4, s32[]{:T(128)S(6)} %select_n.9, f32[32]{0:T(128)S(1)} %dynamic_update_slice.27, f32[32]{0:T(128)S(1)} %multiply_add_fusion.3, f32[]{:T(128)} %bitcast, f32[32]{0:T(128)S(1)} %dynamic_update_slice.28), kind=kOutput, calls=%fused_computation.56 | convolution fusion | flops 1048656 | bytes 1181344 | tf_op jit(solution)/shard_map/dot_general | solution.py:30
  75.3 1.7 %fusion.74 = f32[1,65536]{1,0:T(1,128)S(1)} fusion(bf16[32,65536]{1,0:T(8,128)(2,1)} %param.4, s32[]{:T(128)S(6)} %select_n.9, f32[8]{0:T(128)S(1)} %get-tuple-element.14, f32[8]{0:T(128)S(1)} %fusion.47), kind=kOutput, calls=%fused_computation.84 | convolution fusion | flops 1048592 | bytes 1310788 | tf_op jit(solution)/shard_map/dot_general | solution.py:40
  77.0 0.2 add_dynamic-update-slice_fusion.1
  77.2 0.1 reshape.62
  77.4 2.1 %fusion.55 = f32[8]{0:T(128)S(1)} fusion(f32[8]{0:T(128)S(1)} %get-tuple-element.13, bf16[65536,1]{0,1:T(2,128)(2,1)S(1)} %reshape.62, bf16[32,65536]{1,0:T(8,128)(2,1)} %param.4, s32[]{:T(128)S(6)} %select_n.10, f32[32]{0:T(128)S(1)} %dynamic_update_slice.27, f32[32]{0:T(128)S(1)} %multiply_add_fusion.3, f32[]{:T(128)} %bitcast, ...), kind=kOutput, calls=%fused_computation.64 | convolution fusion | flops 1048656 | bytes 1181344 | tf_op jit(solution)/shard_map/dot_general | solution.py:30
  79.4 0.0 copy-done
  79.4 0.4 fusion.68
  79.9 0.2 add_dynamic-update-slice_fusion
  80.1 0.1 add_convert_fusion
  80.2 0.1 reshape.66
  80.3 0.9 fusion.64
  81.2 0.2 dynamic_update_slice.31
  81.4 2.8 %fusion.103 = f32[1,65536]{1,0:T(1,128)S(1)} fusion(bf16[32,65536]{1,0:T(8,128)(2,1)} %param.4, f32[32]{0:T(128)S(1)} %dynamic_update_slice.31, s32[32]{0:T(128)S(1)} %copy-done.1), kind=kOutput, calls=%fused_computation.123 | convolution fusion | flops 4194400 | bytes 4456704 | tf_op jit(solution)/shard_map/dot_general | solution.py:70
  84.2 0.7 broadcast_multiply_fusion
  85.0 0.0 all-gather.7.cloned.1.call-update
  85.0 1.1 fusion.133
  86.1 27.6 %all-gather.7.cloned.1.call-done = f32[524288]{0:T(1024)} async-done(((f32[65536]{0:T(1024)}), f32[524288]{0:T(1024)}) %all-gather.7.cloned.1.call-update) | async-done | bytes 2097168 | tf_op jit(solution)/shard_map/all_gather | solution.py:12
  113.7 2.0 %reshape.35 = f32[8,65536]{1,0:T(8,128)S(1)} reshape(f32[524288]{0:T(1024)} %all-gather.7.cloned.1.call-done) | data formatting | bytes 4194304 | tf_op jit(solution)/shard_map/all_gather | solution.py:12
  115.7 0.5 reduce_sum.46
  116.2 0.7 multiply_reduce_fusion
  116.9 0.1 reshape.70
  117.1 4.5 %maximum_reduce_fusion = (f32[]{:T(128)}, f32[32]{0:T(128)}) fusion(s32[32]{0:T(128)S(1)} %copy-done.1, bf16[65536,1]{0,1:T(2,128)(2,1)S(1)} %reshape.70, bf16[32,65536]{1,0:T(8,128)(2,1)} %param.4), kind=kOutput, calls=%fused_computation.133 | convolution fusion | flops 4194495 | bytes 4325636 | tf_op jit(solution)/shard_map/dot_general | solution.py:74
  121.5 15.9 %all-reduce = (f32[]{:T(128)}, f32[]{:T(128)}) all-reduce(f32[]{:T(128)} %get-tuple-element.16, f32[]{:T(128)} %get-tuple-element.5), channel_id=1, replica_groups=mesh['grp'=4,'blk'=8] {'blk'}, use_global_device_ids=true, to_apply=%region_4.5 | all-reduce | flops 2 | bytes 16 | tf_op jit(solution)/shard_map/psum | solution.py:78
  (8 shorter events, 0.2 us)
Async XLA Ops:
  7.2 59.1 %all-gather.5.cloned.1.call-start = ((), (), s32[]{:S(2)}) async-start(), calls=%async_computation | async-start | bytes 2359296 | tf_op jit(solution)/shard_map/all_gather | solution.py:12
  21.5 9.1 %copy-start.1 = (s32[32]{0:T(128)S(1)}, s32[32]{0:T(128)}, u32[]{:S(2)}) copy-start(s32[32]{0:T(128)} %param.5) | copy-start | bytes 388
  34.3 79.4 %all-gather.7.cloned.1.call-start = ((), (), s32[]{:S(2)}) async-start(), calls=%async_computation.1 | async-start | bytes 2359296 | tf_op jit(solution)/shard_map/all_gather | solution.py:12
  73.1 6.3 %copy-start = (bf16[32,65536]{1,0:T(8,128)(2,1)S(1)}, bf16[32,65536]{1,0:T(8,128)(2,1)}, u32[]{:S(2)}) copy-start(bf16[32,65536]{1,0:T(8,128)(2,1)} %param.4) | copy-start | bytes 12582916
Sparse Core Ops, SparseCore 0:
  34.4 31.8 all-gather.4
  85.1 28.5 all-gather.6
